TPU v7x, 512 devices: a whole 4x4x16 slice. The times are simulated.
512 devices in a mesh: dp: 4 (over y), tensor: 8 (over z_hi, x), enc: 16 (over z_lo, core).
Axes of the slice: x: 4, y: 4, z: 16 (z_hi: 2, z_lo: 8; z = z_hi * 8 + z_lo), core: 2. Of those that a mesh axis runs over, the one named last changes fastest.
Arguments:
- span_states: bfloat16 [8192, 8192], P(('dp', 'enc'), 'tensor'), may hold values from -6 to 6
- neighbours: bfloat16 [128, 256, 1024], P(('dp', 'enc'), None, 'tensor'), may hold values from -6 to 6
- lengths: int32 [4], P('dp'), may hold values from 1 to 2048, 4096 in all
- wq_enc: bfloat16 [1024, 1024], P('enc', 'tensor')
- wk_enc: bfloat16 [8192, 1024], P('enc', 'tensor'), may hold values from -0.0625 to 0.0625
- wv_enc: bfloat16 [8192, 1024], P('enc', 'tensor'), may hold values from -0.0625 to 0.0625
- wo_enc: bfloat16 [1024, 1024], P('enc', 'tensor'), may hold values from -0.1875 to 0.1875
- wk_dec: bfloat16 [1024, 8192], P(('dp', 'enc'), 'tensor'), may hold values from -0.1875 to 0.1875
- wv_dec: bfloat16 [1024, 8192], P(('dp', 'enc'), 'tensor'), may hold values from -0.1875 to 0.1875
- queries: bfloat16 [8192, 8192], P(('dp', 'enc'), 'tensor'), may hold values from -6 to 6
- grad_out: bfloat16 [8192, 8192], P(('dp', 'enc'), 'tensor'), may hold values from -6 to 6
Outputs:
- attended: bfloat16 [8192, 8192], P(('dp', 'enc'), 'tensor')
- grad_encoded: float32 [128, 256, 1024], P(('dp', 'enc'), None, 'tensor')
Inputs may be any that keep to these rules, and one draw needn't show every extreme that they name: `lengths`: some sequence is live over all 2048 tokens.
All inputs are finite; a program needn't handle non-finite values. No bound on the sum of `lengths` on one device may be relied on, other than what follows from the above.
Results may differ from a plain program's by a relative error of at most 0.019.
Values may be sent and summed in bfloat16 or wider, within the bound.
A program may use at most 64 MiB of HBM per device.

v0:
```python
import math
import jax
import jax.numpy as jnp
from jax import lax
from jax.sharding import Mesh
from jax.sharding import PartitionSpec as P

HD = 128
EH = 64
TENSOR = ("tensor_0", "tensor_1")


def in_order(blocks, dim):
    dims = list(blocks.shape[1:])
    dims[dim] *= blocks.shape[0]
    return jnp.moveaxis(blocks, 0, dim).reshape(dims)


def one_gather(arrays, axis, dims):
    vector = jnp.concatenate([a.reshape(-1) for a in arrays])
    lines, at, gathered = (lax.all_gather(vector, axis), 0, [])
    for a, dim in zip(arrays, dims):
        blocks = lines[:, at : at + a.size].reshape(-1, *a.shape)
        gathered.append(in_order(blocks, dim))
        at += a.size
    return tuple(gathered)


def copy_for_each(x, axis):
    copies = jnp.broadcast_to(x, (lax.axis_size(axis), *x.shape))
    return lax.all_to_all(copies, axis, split_axis=0, concat_axis=0, tiled=True)


def gathered_copies(x, axis, dim):
    blocks = copy_for_each(x, axis)
    return in_order(blocks, dim)


def in_one_piece(arrays, axis, dim, along):
    both = jnp.concatenate(arrays, axis=along)
    filled, at, gathered = (lax.all_gather(both, axis, axis=dim, tiled=True), 0, [])
    for a in arrays:
        gathered.append(lax.slice_in_dim(filled, at, at + a.shape[along], axis=along))
        at += a.shape[along]
    return tuple(gathered)


def from_behind(value, axis, steps):
    count = lax.axis_size(axis)
    first, last = (max(0, -steps), min(count, count - steps))
    return lax.ppermute(value, axis, [(source, source + steps) for source in range(first, last)])


def sum_in_order(blocks, axes, turns):
    inside = blocks.shape[1:]
    blocks = blocks.reshape(*(lax.axis_size(a) for a in axes), *inside)
    blocks = jnp.moveaxis(blocks, turns, range(len(axes))).reshape(-1, *inside)
    for k in turns:
        blocks = lax.psum_scatter(blocks, axes[k], scatter_dimension=0, tiled=True)
    return blocks[0]


def in_blocks(x, dim, count):
    before, after = (x.shape[:dim], x.shape[dim + 1 :])
    return jnp.moveaxis(x.reshape(*before, count, -1, *after), dim, 0)


def summed_rows(x, axes, turns, dim):
    count = lax.axis_size(axes)
    return sum_in_order(in_blocks(x, dim, count), axes, turns)


def on_device(
    span_states,
    neighbours,
    lengths,
    wq_enc,
    wk_enc,
    wv_enc,
    wo_enc,
    wk_dec,
    wv_dec,
    queries,
    grad_out,
):
    spans, keys_each, width = neighbours.shape
    row_count = span_states.shape[0]
    span_len = row_count // spans
    key_rows = spans * keys_each
    flat_neighbour = neighbours.reshape(key_rows, width)
    full_states, full_neighbour = one_gather((span_states, flat_neighbour), TENSOR, (1, 1))
    sliced = full_neighbour
    query_sum = jnp.dot(
        sliced, gathered_copies(wq_enc, "enc", 0), preferred_element_type=jnp.float32
    )
    segments = in_one_piece((wk_enc, wv_enc), "enc", 0, 1)
    sliced = full_states
    key_sum = jnp.dot(sliced, segments[0], preferred_element_type=jnp.float32)
    value_sum = jnp.dot(sliced, segments[1], preferred_element_type=jnp.float32)
    heads_enc = width // EH
    query_heads = query_sum.astype(jnp.bfloat16).reshape(spans, keys_each, heads_enc, EH)
    key_heads = key_sum.astype(jnp.bfloat16).reshape(spans, span_len, heads_enc, EH)
    value_heads = value_sum.astype(jnp.bfloat16).reshape(spans, span_len, heads_enc, EH)
    scores = jnp.einsum(
        "cqhe,ckhe->chqk", query_heads, key_heads, preferred_element_type=jnp.float32
    ) / math.sqrt(EH)
    enc_weights = jax.nn.softmax(scores, axis=-1).astype(jnp.bfloat16)
    head_mix = jnp.einsum(
        "chqk,ckhe->cqhe", enc_weights, value_heads, preferred_element_type=jnp.float32
    )
    head_mix = head_mix.astype(jnp.bfloat16).reshape(key_rows, width)
    full_mix = lax.all_gather(head_mix, TENSOR, axis=1, tiled=True)
    sliced = full_mix
    output_sum = jnp.dot(
        sliced, gathered_copies(wo_enc, "enc", 0), preferred_element_type=jnp.float32
    )
    encoded = (
        (flat_neighbour.astype(jnp.float32) + output_sum)
        .astype(jnp.bfloat16)
        .reshape(spans, keys_each, width)
    )
    carried = from_behind(encoded[spans - 1], "enc", 1)
    previous_part = jnp.concatenate([carried[None], encoded[: spans - 1]], axis=0).reshape(
        key_rows, width
    )
    previous = lax.all_gather(previous_part, TENSOR, axis=1, tiled=True)
    key_weight, value_weight = in_one_piece((wk_dec, wv_dec), ("dp", "enc"), 0, 1)
    dec_key = jnp.dot(previous, key_weight, preferred_element_type=jnp.float32).astype(jnp.bfloat16)
    dec_value = jnp.dot(previous, value_weight, preferred_element_type=jnp.float32).astype(
        jnp.bfloat16
    )
    heads_dec = queries.shape[1] // HD
    query_dec = queries.reshape(spans, span_len, heads_dec, HD)
    key_dec = dec_key.reshape(spans, keys_each, heads_dec, HD)
    value_dec = dec_value.reshape(spans, keys_each, heads_dec, HD)
    dec_scores = jnp.einsum(
        "cmhd,ckhd->chmk", query_dec, key_dec, preferred_element_type=jnp.float32
    ) / math.sqrt(HD)
    probs = jax.nn.softmax(dec_scores, axis=-1)
    probs_low = probs.astype(jnp.bfloat16)
    position = lax.axis_index("enc") * row_count + jnp.arange(row_count, dtype=jnp.int32)
    live_mask = jnp.logical_and(position < lengths[0], position >= span_len).reshape(
        spans, span_len, 1, 1
    )
    attended = jnp.einsum(
        "chmk,ckhd->cmhd", probs_low, value_dec, preferred_element_type=jnp.float32
    )
    attended = jnp.where(live_mask, attended, 0.0).astype(jnp.bfloat16).reshape(row_count, -1)
    cotangent = jnp.where(
        live_mask, grad_out.reshape(spans, span_len, heads_dec, HD), jnp.zeros((), jnp.bfloat16)
    )
    grad_value = jnp.einsum(
        "chmk,cmhd->ckhd", probs_low, cotangent, preferred_element_type=jnp.float32
    ).astype(jnp.bfloat16)
    grad_probs = jnp.einsum(
        "cmhd,ckhd->chmk", cotangent, value_dec, preferred_element_type=jnp.float32
    )
    inner = jnp.sum(grad_probs * probs, axis=-1, keepdims=True)
    grad_scores = (probs * (grad_probs - inner) / math.sqrt(HD)).astype(jnp.bfloat16)
    grad_key = jnp.einsum(
        "chmk,cmhd->ckhd", grad_scores, query_dec, preferred_element_type=jnp.float32
    ).astype(jnp.bfloat16)
    partial_value = jnp.einsum(
        "nd,ed->ne", grad_key.reshape(key_rows, -1), key_weight, preferred_element_type=jnp.float32
    )
    partial_value = partial_value + jnp.einsum(
        "nd,ed->ne",
        grad_value.reshape(key_rows, -1),
        value_weight,
        preferred_element_type=jnp.float32,
    )
    returned = (
        summed_rows(partial_value.astype(jnp.bfloat16), TENSOR, (1, 0), 1)
        .astype(jnp.float32)
        .reshape(spans, keys_each, width)
    )
    following = from_behind(returned[0].astype(jnp.bfloat16), "enc", -1).astype(jnp.float32)
    grad_encoded = jnp.concatenate([returned[1:], following[None]], axis=0)
    return (attended, grad_encoded)


def solution(mesh):
    split = Mesh(
        mesh.devices.reshape(mesh.shape["dp"], 2, 4, mesh.shape["enc"]),
        ("dp", "tensor_0", "tensor_1", "enc"),
    )
    in_specs = (
        P(("dp", "enc"), TENSOR),
        P(("dp", "enc"), None, TENSOR),
        P("dp"),
        P("enc", TENSOR),
        P("enc", TENSOR),
        P("enc", TENSOR),
        P("enc", TENSOR),
        P(("dp", "enc"), TENSOR),
        P(("dp", "enc"), TENSOR),
        P(("dp", "enc"), TENSOR),
        P(("dp", "enc"), TENSOR),
    )
    out_specs = (P(("dp", "enc"), TENSOR), P(("dp", "enc"), None, TENSOR))
    return jax.shard_map(
        on_device, mesh=split, in_specs=in_specs, out_specs=out_specs, check_vma=False
    )
```

profile of v0, /device:TPU:1, one launch (start us, length us, event | category | flops | bytes accessed | tf_op | source)
XLA Modules:
  0.0 678.9 jit_solution(7648377399311561809)
XLA Ops:
  7.2 0.0 all-gather.15.cloned.1.call-start
  7.2 1.0 copy.55
  8.2 1.7 pad_maximum_fusion
  9.9 0.0 all-gather.15.cloned.1.call-update
  9.9 0.0 all-gather.7.cloned.1.call-start
  10.0 1.7 pad_maximum_fusion.1
  11.7 0.8 broadcast_in_dim.43
  12.5 14.0 %all-to-all-start = ((bf16[16,64,128]{2,1,0:T(8,128)(2,1)}), bf16[16,64,128]{2,1,0:T(8,128)(2,1)S(1)}, u32[]{:S(2)}, u32[]{:S(2)}) async-start(bf16[16,64,128]{2,1,0:T(8,128)(2,1)} %broadcast_in_dim.43), calls=%async_computation | async-start | bytes 524288 | tf_op jit(solution)/shard_map/all_to_all | solution.py:31
  26.5 0.0 all-gather.9.cloned.1.call-start
  26.5 135.1 %all-gather.15.cloned.1.call-done = bf16[1572864]{0:T(1024)(128)(2,1)} async-done(((bf16[196608]{0:T(1024)(128)(2,1)}), bf16[1572864]{0:T(1024)(128)(2,1)}) %all-gather.15.cloned.1.call-update) | async-done | bytes 3145744 | tf_op jit(solution)/shard_map/all_gather | solution.py:21
  161.7 3.2 reshape.126
  164.9 1.2 slice.54
  166.1 0.8 copy-done
  166.9 1.8 convolution_convert_fusion.3
  168.7 0.1 reshape.127
  168.9 2.7 copy.56
  171.6 93.4 %all-gather.7.cloned.1.call-done = bf16[8192,256]{1,0:T(8,128)(2,1)} async-done(((bf16[512,256]{1,0:T(8,128)(2,1)}), bf16[8192,256]{1,0:T(8,128)(2,1)}) %all-gather.7.cloned.1.call-update) | async-done | bytes 4194320 | tf_op jit(solution)/shard_map/all_gather | solution.py:41
  265.0 3.1 fusion.50
  268.1 0.1 reshape.111
  268.2 0.2 convolution_multiply_fusion.1
  268.4 0.1 fusion.83
  268.5 2.3 fusion.47
  270.8 0.1 reshape.106
  270.9 0.2 fusion.46
  271.1 0.1 copy.42
  271.3 0.7 copy.58
  272.0 0.0 all-gather.13.cloned.1.call-start
  272.1 0.6 pad_maximum_fusion.3
  272.7 0.0 all-gather.11.cloned.1.call-start
  272.8 27.9 %all_to_all.10 = bf16[16,64,128]{2,1,0:T(8,128)(2,1)S(1)} all-to-all(bf16[16,64,128]{2,1,0:T(8,128)(2,1)S(1)} %broadcast_in_dim.44), channel_id=1, replica_groups=mesh['dp'=4,'tensor_0'=2,'tensor_1'=4,'enc'=16] {'enc'}, dimensions={0} | all-to-all | bytes 524288 | tf_op jit(solution)/shard_map/all_to_all | solution.py:31
  300.8 63.7 %all-gather.9.cloned.1.call-done = bf16[512,1024]{0,1:T(8,128)(2,1)} async-done(((bf16[512,128]{0,1:T(8,128)(2,1)}), bf16[512,1024]{0,1:T(8,128)(2,1)}) %all-gather.9.cloned.1.call-update) | async-done | bytes 1048592 | tf_op jit(solution)/shard_map/all_gather | solution.py:112
  364.5 1.7 fusion.45
  366.2 1.9 collective-permute-start
  368.1 2.3 collective-permute-done
  370.4 0.7 pad_maximum_fusion.2
  371.1 0.2 reduce-scatter.3.cloned.1.call-start
  372.2 109.5 %all-gather.13.cloned.1.call-done = bf16[1024,2048]{1,0:T(8,128)(2,1)} async-done(((bf16[16,2048]{1,0:T(8,128)(2,1)}), bf16[1024,2048]{1,0:T(8,128)(2,1)}) %all-gather.13.cloned.1.call-update) | async-done | bytes 4194320 | tf_op jit(solution)/shard_map/all_gather | solution.py:41
  481.6 85.6 %all-gather.11.cloned.1.call-done = bf16[512,1024]{1,0:T(8,128)(2,1)} async-done(((bf16[512,128]{1,0:T(8,128)(2,1)}), bf16[512,1024]{1,0:T(8,128)(2,1)}) %all-gather.11.cloned.1.call-update) | async-done | bytes 1048592 | tf_op jit(solution)/shard_map/all_gather | solution.py:126
  567.2 3.3 fusion.27
  570.5 0.3 copy.61
  570.8 0.9 copy-done.13
  571.7 1.3 fusion.30
  573.0 0.3 copy.59
  573.3 0.5 fusion.39
  573.8 1.2 fusion.84
  575.0 3.2 fusion.25
  578.1 2.4 copy.51
  580.6 1.5 fusion.62
  582.1 8.7 %fusion.24 = bf16[2,256,8,128]{3,1,2,0:T(8,128)(2,1)} fusion(f32[2,8,64,256]{3,2,1,0:T(8,128)S(1)} %fusion.62, bf16[2,64,8,128]{3,2,1,0:T(8,128)(2,1)S(1)} %bitcast.103, f32[2,8,64,256]{3,2,1,0:T(8,128)} %get-tuple-element.7, f32[2,8,64]{2,1,0:T(8,128)S(1)} %get-tuple-element.6), kind=kOutput, calls=%fused_computation.21 | convolution fusion | flops 69469440 | bytes 3411968 | tf_op jit(solution)/shard_map/chmk,cmhd->ckhd/dot_general | solution.py:160
  590.8 2.0 copy.50
  592.8 3.0 fusion.7
  595.8 1.3 fusion.33
  597.1 0.3 copy.66
  597.4 1.2 copy.52
  598.6 0.0 reduce-scatter.5.cloned.1.call-start
  598.7 22.4 %reduce-scatter.3.cloned.1.call-done = bf16[2,512,128]{2,1,0:T(8,128)(2,1)} async-done(((bf16[8,512,128]{2,1,0:T(8,128)(2,1)}), bf16[2,512,128]{2,1,0:T(8,128)(2,1)}) %reduce-scatter.3.cloned.1.call-update) | async-done | bytes 262160 | tf_op jit(solution)/shard_map/reduce_scatter | solution.py:59
  621.1 43.8 %reduce-scatter.5.cloned.1.call-done = bf16[1,512,128]{2,1,0:T(8,128)(2,1)} async-done(((bf16[2,512,128]{2,1,0:T(8,128)(2,1)}), bf16[1,512,128]{2,1,0:T(8,128)(2,1)}) %reduce-scatter.5.cloned.1.call-update) | async-done | bytes 131088 | tf_op jit(solution)/shard_map/reduce_scatter | solution.py:59
  664.9 0.9 fusion.81
  665.8 2.6 collective-permute-start.1
  668.4 1.9 fusion.43
  670.3 0.2 copy.46
  670.4 0.8 copy.99
  671.2 0.1 collective-permute-done.1
  671.3 0.7 maximum_convert_fusion
  (40 shorter events, 0.3 us)
Async XLA Ops:
  7.2 4.5 copy-start.9
  7.2 154.5 %all-gather.15.cloned.1.call-start = ((), (), s32[]{:S(2)}) async-start(), calls=%async_computation.10 | async-start | bytes 3538944 | tf_op jit(solution)/shard_map/all_gather | solution.py:21
  9.9 255.1 %all-gather.7.cloned.1.call-start = ((), (), s32[]{:S(2)}) async-start(), calls=%async_computation.4 | async-start | bytes 4456448 | tf_op jit(solution)/shard_map/all_gather | solution.py:41
  12.5 154.4 %all-to-all-start = ((bf16[16,64,128]{2,1,0:T(8,128)(2,1)}), bf16[16,64,128]{2,1,0:T(8,128)(2,1)S(1)}, u32[]{:S(2)}, u32[]{:S(2)}) async-start(bf16[16,64,128]{2,1,0:T(8,128)(2,1)} %broadcast_in_dim.43), calls=%async_computation | async-start | bytes 524288 | tf_op jit(solution)/shard_map/all_to_all | solution.py:31
  26.5 338.0 %all-gather.9.cloned.1.call-start = ((), (), s32[]{:S(2)}) async-start(), calls=%async_computation.5 | async-start | bytes 1179648 | tf_op jit(solution)/shard_map/all_gather | solution.py:112
  164.9 2.0 copy-start
  166.9 2.0 slice-start
  265.0 3.5 copy-start.1
  268.5 3.6 copy-start.7
  268.5 3.6 copy-start.8
  270.8 2.0 copy-start.10
  270.8 93.7 %copy-start.4 = (bf16[2,256,128]{2,1,0:T(8,128)(2,1)S(1)}, bf16[2,256,128]{2,1,0:T(8,128)(2,1)}, u32[]{:S(2)}) copy-start(bf16[2,256,128]{2,1,0:T(8,128)(2,1)} %param.12) | copy-start | bytes 393220
  271.1 100.9 %copy-start.5 = (bf16[128,1024]{1,0:T(8,128)(2,1)S(1)}, bf16[128,1024]{1,0:T(8,128)(2,1)}, u32[]{:S(2)}) copy-start(bf16[128,1024]{1,0:T(8,128)(2,1)} %param.20) | copy-start | bytes 786436
  271.3 100.8 %copy-start.6 = (bf16[128,1024]{1,0:T(8,128)(2,1)S(1)}, bf16[128,1024]{1,0:T(8,128)(2,1)}, u32[]{:S(2)}) copy-start(bf16[128,1024]{1,0:T(8,128)(2,1)} %param.21) | copy-start | bytes 786436
  272.0 209.6 %all-gather.13.cloned.1.call-start = ((), (), s32[]{:S(2)}) async-start(), calls=%async_computation.7 | async-start | bytes 4259840 | tf_op jit(solution)/shard_map/all_gather | solution.py:41
  272.7 294.5 %all-gather.11.cloned.1.call-start = ((), (), s32[]{:S(2)}) async-start(), calls=%async_computation.6 | async-start | bytes 1179648 | tf_op jit(solution)/shard_map/all_gather | solution.py:126
  366.2 4.2 collective-permute-start
  371.1 249.9 %reduce-scatter.3.cloned.1.call-start = ((), (), s32[]{:S(2)}) async-start(), calls=%async_computation.8 | async-start | bytes 1310720 | tf_op jit(solution)/shard_map/reduce_scatter | solution.py:59
  372.1 202.9 %copy-start.2 = (bf16[16,8,8,128]{3,2,1,0:T(8,128)(2,1)}, bf16[16,8,8,128]{3,2,1,0:T(8,128)(2,1)S(1)}, u32[]{:S(2)}) copy-start(bf16[16,8,8,128]{3,2,1,0:T(8,128)(2,1)S(1)} %copy.63) | copy-start | bytes 786436
  567.2 3.6 copy-start.11
  570.5 1.2 copy-start.13
  590.8 2.0 copy-start.3
  592.8 3.0 copy-start.12
  598.6 66.3 %reduce-scatter.5.cloned.1.call-start = ((), (), s32[]{:S(2)}) async-start(), calls=%async_computation.9 | async-start | bytes 393216 | tf_op jit(solution)/shard_map/reduce_scatter | solution.py:59
  665.8 5.6 collective-permute-start.1
Sparse Core Ops, SparseCore 0:
  11.2 150.4 all-gather.14
  164.3 100.6 all-gather.6
  272.1 92.2 all-gather.8
  366.5 115.0 all-gather.12
  485.1 82.0 all-gather.10
  598.7 22.2 reduce-scatter.2
  623.8 40.9 reduce-scatter.4
where the time goes:
time: 680 us; the launch traced here: 679 us
  waiting for transfers between devices  556 us (82%)
  matrix products  33.9 us (5%)
  blocking collectives  27.9 us (4%)
  local copies, waits for them, and re-layouts  20.2 us (3%)
  starting transfers between devices  19 us (3%)
  between operations  15.2 us (2%)
    all_gather x2, waiting for transfers between devices, in_one_piece(): lax.all_gather(both, axis, axis=dim, tiled=True)  203 us
    all_gather x1, waiting for transfers between devices, one_gather(): lines, at, gathered = (lax.all_gather(vector, axis), 0, [])  135 us
    all_gather x1, waiting for transfers between devices, on_device(): previous = lax.all_gather(previous_part, TENSOR, axis=1, tiled=True)  85.6 us
    reduce_scatter x2, waiting for transfers between devices, sum_in_order(): blocks = lax.psum_scatter(blocks, axes[k], scatter_dimension=0, tiled=True)  66.2 us
    all_gather x1, waiting for transfers between devices, on_device(): full_mix = lax.all_gather(head_mix, TENSOR, axis=1, tiled=True)  63.7 us
    all_to_all x1, blocking collectives, copy_for_each(): return lax.all_to_all(copies, axis, split_axis=0, concat_axis=0, tiled=True)  27.9 us
    all_to_all x1, starting transfers between devices, copy_for_each(): return lax.all_to_all(copies, axis, split_axis=0, concat_axis=0, tiled=True)  14 us
  transfers between devices with their start and end apart: 10, of which 9 were waited for; matrix products, arithmetic and copies ran while one was open for 3% of the time, Pallas kernels for 0%

commit v1 on v0

--- a/solution.py
+++ b/solution.py
@@ -109,7 +109,8 @@
         "chqk,ckhe->cqhe", enc_weights, value_heads, preferred_element_type=jnp.float32
     )
     head_mix = head_mix.astype(jnp.bfloat16).reshape(key_rows, width)
-    full_mix = lax.all_gather(head_mix, TENSOR, axis=1, tiled=True)
+    sent = jnp.stack([head_mix] * lax.axis_size(TENSOR))
+    full_mix = jnp.concatenate(lax.all_to_all(sent, TENSOR, 0, 0), axis=1)
     sliced = full_mix
     output_sum = jnp.dot(
         sliced, gathered_copies(wo_enc, "enc", 0), preferred_element_type=jnp.float32

time: 680 us -> 612 us (0.900)
  waiting for transfers between devices: 556 us -> 460 us
  blocking collectives: 27.9 us -> 47.9 us
  starting transfers between devices: 19 us -> 28.8 us
    all_gather x1 -> x0, waiting for transfers between devices: 63.7 us -> none  [on_device(): full_mix = lax.all_gather(head_mix, TENSOR, axis=1, tiled=True)]
    all_gather x2, waiting for transfers between devices: 203 us -> 172 us  [in_one_piece(): lax.all_gather(both, axis, axis=dim, tiled=True)]
    all_to_all x1, blocking collectives: 27.9 us -> 47.9 us  [on_device(): full_mix = jnp.concatenate(lax.all_to_all(sent, TENSOR, 0, 0), axis=1)]
    all_to_all x1 -> x2, starting transfers between devices: 14 us -> 23.9 us  [copy_for_each(): return lax.all_to_all(copies, axis, split_axis=0, concat_axis=0, tiled=True)]
  transfers between devices with their start and end apart: 10 -> 10, of which waited for: 9 -> 8; matrix products, arithmetic and copies ran while one was open for 3% -> 4% of each run, Pallas kernels for 0% -> 0%
where the time goes in v1:
time: 612 us
  waiting for transfers between devices  460 us (75%)
  blocking collectives  47.9 us (8%)
  matrix products  32.6 us (5%)
  starting transfers between devices  28.8 us (5%)
  local copies, waits for them, and re-layouts  20.3 us (3%)
  between operations  15.2 us (2%)
  other arithmetic  6.67 us (1%)
    all_gather x2, waiting for transfers between devices, in_one_piece(): lax.all_gather(both, axis, axis=dim, tiled=True)  172 us
    all_gather x1, waiting for transfers between devices, one_gather(): lines, at, gathered = (lax.all_gather(vector, axis), 0, [])  135 us
    all_gather x1, waiting for transfers between devices, on_device(): previous = lax.all_gather(previous_part, TENSOR, axis=1, tiled=True)  85.2 us
    reduce_scatter x2, waiting for transfers between devices, sum_in_order(): blocks = lax.psum_scatter(blocks, axes[k], scatter_dimension=0, tiled=True)  66 us
    all_to_all x1, blocking collectives, on_device(): full_mix = jnp.concatenate(lax.all_to_all(sent, TENSOR, 0, 0), axis=1)  47.9 us
    all_to_all x2, starting transfers between devices, copy_for_each(): return lax.all_to_all(copies, axis, split_axis=0, concat_axis=0, tiled=True)  23.9 us
  transfers between devices with their start and end apart: 10, of which 8 were waited for; matrix products, arithmetic and copies ran while one was open for 4% of the time, Pallas kernels for 0%

profile of v1, /device:TPU:1, one launch (start us, length us, event | category | flops | bytes accessed | tf_op | source)
XLA Modules:
  0.0 611.7 jit_solution(5138663553229847480)
XLA Ops:
  7.2 0.0 all-gather.12.cloned.1.call-start
  7.2 1.0 copy.55
  8.2 1.7 pad_maximum_fusion
  9.9 0.0 all-gather.6.cloned.1.call-start
  10.0 1.7 pad_maximum_fusion.1
  11.7 0.0 all-gather.10.cloned.1.call-start
  11.8 0.6 pad_maximum_fusion.3
  12.4 0.0 all-gather.10.cloned.1.call-update
  12.5 0.8 broadcast_in_dim.43
  13.2 14.0 %all-to-all-start = ((bf16[16,64,128]{2,1,0:T(8,128)(2,1)}), bf16[16,64,128]{2,1,0:T(8,128)(2,1)S(1)}, u32[]{:S(2)}, u32[]{:S(2)}) async-start(bf16[16,64,128]{2,1,0:T(8,128)(2,1)} %broadcast_in_dim.43), calls=%async_computation | async-start | bytes 524288 | tf_op jit(solution)/shard_map/all_to_all | solution.py:31
  27.2 135.2 %all-gather.12.cloned.1.call-done = bf16[1572864]{0:T(1024)(128)(2,1)} async-done(((bf16[196608]{0:T(1024)(128)(2,1)}), bf16[1572864]{0:T(1024)(128)(2,1)}) %all-gather.12.cloned.1.call-update) | async-done | bytes 3145744 | tf_op jit(solution)/shard_map/all_gather | solution.py:21
  162.5 3.2 reshape.132
  165.7 1.1 slice.54
  166.8 0.8 copy-done
  167.7 0.8 broadcast_in_dim.44
  168.4 9.8 %all-to-all-start.2 = ((bf16[16,64,128]{2,1,0:T(8,128)(2,1)}), bf16[16,64,128]{2,1,0:T(8,128)(2,1)S(1)}, u32[]{:S(2)}, u32[]{:S(2)}) async-start(bf16[16,64,128]{2,1,0:T(8,128)(2,1)} %broadcast_in_dim.44), calls=%async_computation.2 | async-start | bytes 524288 | tf_op jit(solution)/shard_map/all_to_all | solution.py:31
  178.3 0.0 all-gather.8.cloned.1.call-start
  178.3 1.7 convolution_convert_fusion.3
  180.0 0.1 reshape.133
  180.2 2.8 copy.56
  182.9 85.2 %all-gather.6.cloned.1.call-done = bf16[8192,256]{1,0:T(8,128)(2,1)} async-done(((bf16[512,256]{1,0:T(8,128)(2,1)}), bf16[8192,256]{1,0:T(8,128)(2,1)}) %all-gather.6.cloned.1.call-update) | async-done | bytes 4194320 | tf_op jit(solution)/shard_map/all_gather | solution.py:41
  268.1 3.1 fusion.50
  271.2 0.1 reshape.116
  271.3 2.3 fusion.47
  273.6 0.1 reshape.111
  273.7 0.2 convolution_multiply_fusion.1
  273.9 0.1 fusion.83
  274.0 0.2 fusion.46
  274.2 0.1 copy.42
  274.4 0.1 stack.3
  274.5 47.9 %all_to_all.15 = bf16[8,512,128]{1,2,0:T(8,128)(2,1)S(1)} all-to-all(bf16[8,512,128]{1,2,0:T(8,128)(2,1)S(1)} %stack.3), channel_id=1, replica_groups=mesh['dp'=4,'tensor_0'=2,'tensor_1'=4,'enc'=16] {'tensor_0','tensor_1'}, dimensions={0} | all-to-all | bytes 2097152 | tf_op jit(solution)/shard_map/all_to_all | solution.py:113
  322.4 0.5 fusion.45
  322.9 1.9 collective-permute-start
  324.8 1.3 collective-permute-done
  326.1 0.7 pad_maximum_fusion.2
  326.8 0.2 reduce-scatter.3.cloned.1.call-start
  327.8 87.1 %all-gather.10.cloned.1.call-done = bf16[1024,2048]{1,0:T(8,128)(2,1)} async-done(((bf16[16,2048]{1,0:T(8,128)(2,1)}), bf16[1024,2048]{1,0:T(8,128)(2,1)}) %all-gather.10.cloned.1.call-update) | async-done | bytes 4194320 | tf_op jit(solution)/shard_map/all_gather | solution.py:41
  415.0 85.2 %all-gather.8.cloned.1.call-done = bf16[512,1024]{1,0:T(8,128)(2,1)} async-done(((bf16[512,128]{1,0:T(8,128)(2,1)}), bf16[512,1024]{1,0:T(8,128)(2,1)}) %all-gather.8.cloned.1.call-update) | async-done | bytes 1048592 | tf_op jit(solution)/shard_map/all_gather | solution.py:127
  500.2 3.3 fusion.27
  503.5 0.3 copy.61
  503.8 0.9 copy-done.13
  504.7 1.3 fusion.30
  506.0 0.3 copy.59
  506.2 0.5 fusion.39
  506.7 1.2 fusion.84
  507.9 3.2 fusion.25
  511.1 2.4 copy.51
  513.5 1.5 fusion.62
  515.0 8.7 %fusion.24 = bf16[2,256,8,128]{3,1,2,0:T(8,128)(2,1)} fusion(f32[2,8,64,256]{3,2,1,0:T(8,128)S(1)} %fusion.62, bf16[2,64,8,128]{3,2,1,0:T(8,128)(2,1)S(1)} %bitcast.107, f32[2,8,64,256]{3,2,1,0:T(8,128)} %get-tuple-element.7, f32[2,8,64]{2,1,0:T(8,128)S(1)} %get-tuple-element.6), kind=kOutput, calls=%fused_computation.21 | convolution fusion | flops 69469440 | bytes 3411968 | tf_op jit(solution)/shard_map/chmk,cmhd->ckhd/dot_general | solution.py:161
  523.7 2.0 copy.50
  525.7 3.0 fusion.7
  528.8 1.3 fusion.33
  530.1 0.3 copy.66
  530.3 1.1 copy.52
  531.5 0.0 reduce-scatter.5.cloned.1.call-start
  531.6 22.4 %reduce-scatter.3.cloned.1.call-done = bf16[2,512,128]{2,1,0:T(8,128)(2,1)} async-done(((bf16[8,512,128]{2,1,0:T(8,128)(2,1)}), bf16[2,512,128]{2,1,0:T(8,128)(2,1)}) %reduce-scatter.3.cloned.1.call-update) | async-done | bytes 262160 | tf_op jit(solution)/shard_map/reduce_scatter | solution.py:59
  554.0 43.6 %reduce-scatter.5.cloned.1.call-done = bf16[1,512,128]{2,1,0:T(8,128)(2,1)} async-done(((bf16[2,512,128]{2,1,0:T(8,128)(2,1)}), bf16[1,512,128]{2,1,0:T(8,128)(2,1)}) %reduce-scatter.5.cloned.1.call-update) | async-done | bytes 131088 | tf_op jit(solution)/shard_map/reduce_scatter | solution.py:59
  597.6 0.9 fusion.81
  598.5 2.6 collective-permute-start.1
  601.1 1.9 fusion.43
  603.0 0.2 copy.46
  603.2 0.8 copy.99
  604.0 0.1 collective-permute-done.1
  604.1 0.7 maximum_convert_fusion
  (40 shorter events, 0.3 us)
Async XLA Ops:
  7.2 4.6 copy-start.7
  7.2 4.6 copy-start.8
  7.2 5.3 copy-start.9
  7.2 155.3 %all-gather.12.cloned.1.call-start = ((), (), s32[]{:S(2)}) async-start(), calls=%async_computation.10 | async-start | bytes 3538944 | tf_op jit(solution)/shard_map/all_gather | solution.py:21
  9.9 258.2 %all-gather.6.cloned.1.call-start = ((), (), s32[]{:S(2)}) async-start(), calls=%async_computation.5 | async-start | bytes 4456448 | tf_op jit(solution)/shard_map/all_gather | solution.py:41
  11.7 403.2 %all-gather.10.cloned.1.call-start = ((), (), s32[]{:S(2)}) async-start(), calls=%async_computation.7 | async-start | bytes 4259840 | tf_op jit(solution)/shard_map/all_gather | solution.py:41
  13.2 154.5 %all-to-all-start = ((bf16[16,64,128]{2,1,0:T(8,128)(2,1)}), bf16[16,64,128]{2,1,0:T(8,128)(2,1)S(1)}, u32[]{:S(2)}, u32[]{:S(2)}) async-start(bf16[16,64,128]{2,1,0:T(8,128)(2,1)} %broadcast_in_dim.43), calls=%async_computation | async-start | bytes 524288 | tf_op jit(solution)/shard_map/all_to_all | solution.py:31
  165.7 2.0 copy-start
  166.8 0.8 copy-start.10
  167.7 12.5 %slice-start = ((bf16[8,196608]{1,0:T(8,128)(2,1)}), bf16[8,131072]{1,0:T(8,128)(2,1)S(1)}, s32[]{:S(2)}) async-start(bf16[8,196608]{1,0:T(8,128)(2,1)} %copy-done), calls=%async_computation.11 | async-start | bytes 4194304 | tf_op jit(solution)/shard_map/slice | solution.py:23
  168.4 105.9 %all-to-all-start.2 = ((bf16[16,64,128]{2,1,0:T(8,128)(2,1)}), bf16[16,64,128]{2,1,0:T(8,128)(2,1)S(1)}, u32[]{:S(2)}, u32[]{:S(2)}) async-start(bf16[16,64,128]{2,1,0:T(8,128)(2,1)} %broadcast_in_dim.44), calls=%async_computation.2 | async-start | bytes 524288 | tf_op jit(solution)/shard_map/all_to_all | solution.py:31
  178.3 321.9 %all-gather.8.cloned.1.call-start = ((), (), s32[]{:S(2)}) async-start(), calls=%async_computation.6 | async-start | bytes 1179648 | tf_op jit(solution)/shard_map/all_gather | solution.py:127
  268.1 3.2 copy-start.1
  274.2 48.2 %copy-start.4 = (bf16[2,256,128]{2,1,0:T(8,128)(2,1)S(1)}, bf16[2,256,128]{2,1,0:T(8,128)(2,1)}, u32[]{:S(2)}) copy-start(bf16[2,256,128]{2,1,0:T(8,128)(2,1)} %param.12) | copy-start | bytes 393220
  274.5 53.2 %copy-start.5 = (bf16[128,1024]{1,0:T(8,128)(2,1)S(1)}, bf16[128,1024]{1,0:T(8,128)(2,1)}, u32[]{:S(2)}) copy-start(bf16[128,1024]{1,0:T(8,128)(2,1)} %param.20) | copy-start | bytes 786436
  274.5 53.3 %copy-start.6 = (bf16[128,1024]{1,0:T(8,128)(2,1)S(1)}, bf16[128,1024]{1,0:T(8,128)(2,1)}, u32[]{:S(2)}) copy-start(bf16[128,1024]{1,0:T(8,128)(2,1)} %param.21) | copy-start | bytes 786436
  322.9 3.2 collective-permute-start
  326.8 227.2 %reduce-scatter.3.cloned.1.call-start = ((), (), s32[]{:S(2)}) async-start(), calls=%async_computation.8 | async-start | bytes 1310720 | tf_op jit(solution)/shard_map/reduce_scatter | solution.py:59
  327.8 180.1 %copy-start.2 = (bf16[16,8,8,128]{3,2,1,0:T(8,128)(2,1)}, bf16[16,8,8,128]{3,2,1,0:T(8,128)(2,1)S(1)}, u32[]{:S(2)}) copy-start(bf16[16,8,8,128]{3,2,1,0:T(8,128)(2,1)S(1)} %copy.63) | copy-start | bytes 786436
  500.2 3.6 copy-start.11
  503.5 1.2 copy-start.13
  523.7 2.0 copy-start.3
  525.7 3.1 copy-start.12
  531.5 66.1 %reduce-scatter.5.cloned.1.call-start = ((), (), s32[]{:S(2)}) async-start(), calls=%async_computation.9 | async-start | bytes 393216 | tf_op jit(solution)/shard_map/reduce_scatter | solution.py:59
  598.5 5.6 collective-permute-start.1
Sparse Core Ops, SparseCore 0:
  11.2 151.2 all-gather.11
  165.1 102.9 all-gather.5
  270.3 144.6 all-gather.9
  418.4 81.6 all-gather.7
  531.6 22.2 reduce-scatter.2
  556.6 40.9 reduce-scatter.4
